TPU v7x, 32 devices: a whole 2x2x4 slice. The times are simulated.
32 devices in a mesh: group: 4 (over y, x), depth: 2 (over core), mp: 4 (over z).
Axes of the slice: x: 2, y: 2, z: 4, core: 2. Of those that a mesh axis runs over, the one named last changes fastest.
Arguments:
- states: bfloat16 [64, 4096], P(('group', 'depth', 'mp')), may hold values from -6 to 6
- queries: bfloat16 [64, 32, 128], P('group', 'mp'), may hold values from -6 to 6
- new_keys: bfloat16 [64, 8, 128], P('group', 'mp'), may hold values from -18 to 18
- new_values: bfloat16 [64, 8, 128], P('group', 'mp'), may hold values from -24 to 24
- text_keys: bfloat16 [64, 8, 512, 128], P('group', 'mp', 'depth'), may hold values from -6 to 6
- text_values: bfloat16 [64, 8, 512, 128], P('group', 'mp', 'depth'), may hold values from -24 to 24
- text_length: int32 [64], P('group'), may hold values from 2 to 512
- image_keys: bfloat16 [32, 8, 576, 128], P('group', 'mp'), may hold values from -6 to 6
- image_values: bfloat16 [32, 8, 576, 128], P('group', 'mp'), may hold values from -24 to 24
- image_slot: int32 [32], replicated, may hold values from 0 to 31, as said below
- block_list: int32 [4, 32], replicated, may hold values from 0 to 31, as said below
- block_count: int32 [4], replicated, may hold values from 16 to 32, as said below
- image_first: int32 [64], P('group'), may hold values from 0 to 31, as said below
- image_count: int32 [64], P('group'), may hold values from 1 to 2
- out_weight: bfloat16 [4096, 4096], P('mp'), may hold values from -0.09375 to 0.09375
- norm_gain: float32 [4096], replicated, may hold values from 0.5 to 1.5
- gate_weight: bfloat16 [4096, 14336], P(None, ('group', 'mp')), may hold values from -0.09375 to 0.09375
- up_weight: bfloat16 [4096, 14336], P(None, ('group', 'mp')), may hold values from -0.09375 to 0.09375
- down_weight: bfloat16 [14336, 4096], P(('group', 'mp')), may hold values from -0.046875 to 0.046875
Outputs:
- attention: bfloat16 [64, 32, 128], P(('group', 'depth'), 'mp')
- layer_out: bfloat16 [64, 4096], P(('group', 'depth', 'mp'))
Inputs may be any that keep to these rules, and one draw needn't show every extreme that they name: `image_slot`: a permutation. The owner group of hash k is image_slot[k] // 8. `block_list`: the hashes of one group's list are distinct. Among one group's places with the same remainder modulo 2, at most 4 belongs to any one owner group; some group has block_count 32, and there every owner group holds exactly 4 place of every remainder. `block_count`: the sum of image_count over the group's requests. The requests of a group take consecutive list places in request order: image_first is the sum of image_count over the group's earlier requests.
All inputs are finite; a program needn't handle non-finite values.
Results may differ from a plain program's by a relative error of at most 0.012.
Values may be sent and summed in bfloat16 or wider, within the bound.
A program may use at most 128 MiB of HBM per device.

v0:
```python
import math
import jax
import jax.numpy as jnp
from jax import lax
from jax.sharding import PartitionSpec as P

LOG_TWO = math.log(2.0)
MASKED_SCORE = -1e30
NORM_EPSILON = 1e-05


def merged(part, axis, combine):
    gathered = jax.tree.map(lambda a: lax.all_gather(a, axis), part)

    def take(source):
        return jax.tree.map(lambda a: lax.dynamic_index_in_dim(a, source, 0, False), gathered)

    return lax.fori_loop(
        1, lax.axis_size(axis), lambda source, state: combine(state, take(source)), take(0)
    )


def combine(first_part, second_part):
    highest = jnp.maximum(first_part[0], second_part[0])
    first_factor = jnp.exp2(first_part[0] - highest)
    second_factor = jnp.exp2(second_part[0] - highest)
    totals = first_part[1] * first_factor + second_part[1] * second_factor
    weighted = first_part[2] * first_factor[..., None] + second_part[2] * second_factor[..., None]
    return (highest, totals, weighted)


def on_device(
    states,
    queries,
    new_keys,
    new_values,
    text_keys,
    text_values,
    text_length,
    image_keys,
    image_values,
    image_slot,
    block_list,
    block_count,
    image_first,
    image_count,
    out_weight,
    norm_gain,
    gate_weight,
    up_weight,
    down_weight,
):
    groups = lax.axis_size("group")
    depths = lax.axis_size("depth")
    group_index = lax.axis_index("group")
    depth_index = lax.axis_index("depth")
    requests, head_count, head_width = queries.shape
    kv_heads = text_keys.shape[1]
    text_span = text_keys.shape[2]
    stored = image_keys.shape[0]
    listed = block_list.shape[1]
    copies = listed // (depths * groups)
    group_share = head_count // kv_heads
    scaling = 1.0 / math.sqrt(head_width)
    grouped = queries.reshape(requests, kv_heads, group_share, head_width)
    text_scores = (
        jnp.einsum("rhgd,rhpd->rhgp", grouped, text_keys, preferred_element_type=jnp.float32)
        * scaling
    )
    new_scores = (
        jnp.einsum("rhgd,rhd->rhg", grouped, new_keys, preferred_element_type=jnp.float32) * scaling
    )
    positions = depth_index * text_span + jnp.arange(text_span, dtype=jnp.int32)
    text_allowed = (positions[None, :] < text_length[:, None])[:, None, None, :]
    new_allowed = depth_index == 0
    highest = jnp.maximum(
        jnp.max(jnp.where(text_allowed, text_scores, MASKED_SCORE), axis=-1),
        jnp.where(new_allowed, new_scores, MASKED_SCORE),
    )
    levels = jnp.floor(highest / LOG_TWO)
    text_weights = jnp.where(
        text_allowed, jnp.exp(text_scores - LOG_TWO * levels[..., None]), 0.0
    ).astype(jnp.bfloat16)
    new_weights = (
        jnp.where(new_allowed, jnp.exp(new_scores - LOG_TWO * levels), 0.0)
        .astype(jnp.bfloat16)
        .astype(jnp.float32)
    )
    totals = jnp.sum(text_weights, axis=-1, dtype=jnp.float32) + new_weights
    weighted = jnp.einsum(
        "rhgp,rhpd->rhgd", text_weights, text_values, preferred_element_type=jnp.float32
    )
    weighted = weighted + new_weights[..., None] * new_values.astype(jnp.float32)[:, :, None, :]
    local_part = (levels, totals, weighted)

    def owner_table(list_row, list_count, depth):
        indices = jnp.arange(groups * copies, dtype=jnp.int32)
        places = indices * depths + depth
        hashes = jnp.take(list_row, places, axis=0)
        slot_rows = jnp.take(image_slot, hashes, axis=0)
        owners = slot_rows // stored
        within = slot_rows % stored
        active = places < list_count
        member = (
            (owners[:, None] == jnp.arange(groups, dtype=jnp.int32)[None, :]) & active[:, None]
        ).astype(jnp.int32)
        earlier = jnp.cumsum(member, axis=0) - member
        ranked = jnp.sum(earlier * member, axis=1)
        picked = member[:, :, None] * (
            ranked[:, None, None] == jnp.arange(copies, dtype=jnp.int32)[None, None, :]
        ).astype(jnp.int32)
        chosen = jnp.sum(picked * within[:, None, None], axis=0)
        placed = jnp.sum(picked * places[:, None, None], axis=0)
        present = jnp.sum(picked, axis=0) > 0
        return (chosen, placed, present)

    own_row = lax.dynamic_index_in_dim(block_list, group_index, 0, keepdims=False)
    own_count = lax.dynamic_index_in_dim(block_count, group_index, 0, keepdims=False)
    own_chosen, own_placed, own_present = owner_table(own_row, own_count, depth_index)
    finish = image_first + image_count
    in_use = (
        own_present[None]
        & (own_placed[None] >= image_first[:, None, None])
        & (own_placed[None] < finish[:, None, None])
    )
    in_use_int = in_use.astype(jnp.int32)
    every_chosen, every_placed, every_present = jax.vmap(
        lambda list_row, list_count: owner_table(list_row, list_count, depth_index)
    )(block_list, block_count)
    serve_slots = lax.dynamic_index_in_dim(every_chosen, group_index, 1, keepdims=False)
    serve_present = lax.dynamic_index_in_dim(every_present, group_index, 1, keepdims=False)
    request_numbers = jnp.arange(requests, dtype=jnp.int32)[:, None, None]
    reader = jnp.sum(in_use_int * request_numbers, axis=0)
    routed = jnp.take(queries, reader.reshape(-1), axis=0).reshape(
        groups, copies, head_count, head_width
    )
    arrived = lax.all_to_all(routed, "group", split_axis=0, concat_axis=0, tiled=True)
    arrived = arrived.reshape(groups, copies, kv_heads, group_share, head_width)
    owned_keys = jnp.take(image_keys, serve_slots, axis=0)
    owned_values = jnp.take(image_values, serve_slots, axis=0)
    owned_scores = (
        jnp.einsum("schgd,schpd->schgp", arrived, owned_keys, preferred_element_type=jnp.float32)
        * scaling
    )
    owned_allowed = serve_present[:, :, None, None, None]
    owned_high = jnp.max(jnp.where(owned_allowed, owned_scores, MASKED_SCORE), axis=-1)
    owned_levels = jnp.floor(owned_high / LOG_TWO)
    owned_weights = jnp.where(
        owned_allowed, jnp.exp(owned_scores - LOG_TWO * owned_levels[..., None]), 0.0
    ).astype(jnp.bfloat16)
    owned_totals = jnp.sum(owned_weights, axis=-1, dtype=jnp.float32)
    owned_weighted = jnp.einsum(
        "schgp,schpd->schgd", owned_weights, owned_values, preferred_element_type=jnp.float32
    )
    back_levels, back_totals, back_weighted = (
        lax.all_to_all(owned_levels, "group", split_axis=0, concat_axis=0, tiled=True),
        lax.all_to_all(owned_totals, "group", split_axis=0, concat_axis=0, tiled=True),
        lax.all_to_all(owned_weighted, "group", split_axis=0, concat_axis=0, tiled=True),
    )
    use_float = in_use.astype(jnp.float32)
    image_levels = jnp.max(
        jnp.where(in_use[:, :, :, None, None], back_levels[None], MASKED_SCORE), axis=(1, 2)
    )
    image_totals = jnp.einsum(
        "roc,ochg->rhg", use_float, back_totals, precision=lax.Precision.HIGHEST
    )
    image_weighted = jnp.einsum(
        "roc,ochgd->rhgd", use_float, back_weighted, precision=lax.Precision.HIGHEST
    )
    image_part = (image_levels, image_totals, image_weighted)
    partial_value = combine(local_part, image_part)
    merged_levels, merged_totals, merged_weighted = merged(partial_value, "depth", combine)
    attention_all = (
        (merged_weighted / merged_totals[..., None])
        .reshape(requests, head_count, head_width)
        .astype(jnp.bfloat16)
    )
    per_depth = requests // depths
    attention_half = lax.dynamic_slice_in_dim(attention_all, depth_index * per_depth, per_depth, 0)
    flattened = attention_half.reshape(per_depth, head_count * head_width)
    picked_rows = flattened
    projected = lax.psum_scatter(
        jnp.dot(picked_rows, out_weight, preferred_element_type=jnp.float32),
        "mp",
        scatter_dimension=0,
        tiled=True,
    )
    residual = states.astype(jnp.float32) + projected
    spread = jnp.mean(residual * residual, axis=-1, keepdims=True)
    normed = (residual * lax.rsqrt(spread + NORM_EPSILON) * norm_gain).astype(jnp.bfloat16)
    piece = lax.all_gather(normed, ("group", "mp"), axis=0, tiled=True)
    gate_term = jnp.dot(piece, gate_weight, preferred_element_type=jnp.float32)
    up_term = jnp.dot(piece, up_weight, preferred_element_type=jnp.float32)
    hidden = (jax.nn.silu(gate_term) * up_term).astype(jnp.bfloat16)
    picked_rows = hidden
    summed = lax.psum_scatter(
        jnp.dot(picked_rows, down_weight, preferred_element_type=jnp.float32),
        ("group", "mp"),
        scatter_dimension=0,
        tiled=True,
    )
    return (attention_half, (residual + summed).astype(jnp.bfloat16))


def solution(mesh):
    placed = (
        P(("group", "depth", "mp"), None),
        P("group", "mp", None),
        P("group", "mp", None),
        P("group", "mp", None),
        P("group", "mp", "depth", None),
        P("group", "mp", "depth", None),
        P("group"),
        P("group", "mp", None, None),
        P("group", "mp", None, None),
        P(),
        P(),
        P(),
        P("group"),
        P("group"),
        P("mp", None),
        P(),
        P(None, ("group", "mp")),
        P(None, ("group", "mp")),
        P(("group", "mp"), None),
    )
    return jax.shard_map(
        on_device,
        mesh=mesh,
        in_specs=placed,
        out_specs=(P(("group", "depth"), "mp", None), P(("group", "depth", "mp"), None)),
        check_vma=False,
    )
```

profile of v0, /device:TPU:0, one launch (start us, length us, event | category | flops | bytes accessed | tf_op | source)
XLA Modules:
  0.0 287.0 jit_solution(1384392448140040377)
XLA Ops:
  8.8 1.3 gather_fusion.4
  14.6 1.3 gather_fusion.2
  16.6 5.2 %all-to-all-start = ((bf16[4,4,8,128]{3,2,1,0:T(8,128)(2,1)}), bf16[4,4,8,128]{3,2,1,0:T(8,128)(2,1)S(1)}, u32[]{:S(2)}, u32[]{:S(2)}) async-start(bf16[4,4,8,128]{3,2,1,0:T(8,128)(2,1)} %broadcast_select_fusion), calls=%async_computation | async-start | bytes 65536 | tf_op jit(solution)/shard_map/all_to_all | solution.py:137
  24.1 1.4 gather_fusion.1
  27.9 2.3 select_reduce_fusion.1
  31.1 3.3 %gather_fusion.5 = bf16[16,2,576,128]{3,2,1,0:T(8,128)(2,1)} fusion(bf16[8,2,576,128]{3,2,1,0:T(8,128)(2,1)S(1)} %copy-done, s32[1024]{0:T(1024)S(1)} %pad_clamp_fusion), kind=kCustom, calls=%fused_computation.1.clone | custom fusion | bytes 9437248 | tf_op jit(solution)/shard_map/jit(_take)/gather | solution.py:139
  34.5 5.0 %gather_fusion.6 = bf16[16,2,576,128]{3,2,1,0:T(8,128)(2,1)} fusion(bf16[8,2,576,128]{3,2,1,0:T(8,128)(2,1)} %param.31, s32[1024]{0:T(1024)S(1)} %pad_clamp_fusion), kind=kCustom, calls=%fused_computation.3.clone | custom fusion | bytes 9437248 | tf_op jit(solution)/shard_map/jit(_take)/gather | solution.py:140
  39.4 4.0 %select_reduce_fusion = (f32[4,4,2,4]{3,2,1,0:T(2,128)S(1)}, f32[4,4,2,4,576]{4,3,2,1,0:T(4,128)S(1)}) fusion(pred[4,4]{1,0:T(4,128)(4,1)S(1)} %bitcast.98, bf16[4,4,2,4,128]{4,3,2,1,0:T(4,128)(2,1)S(1)} %bitcast.91, bf16[4,4,2,576,128]{4,3,2,1,0:T(8,128)(2,1)} %bitcast.83, pred[4,4]{1,0:T(4,128)(4,1)S(1)} %compare_and_fusion.1), kind=kOutput, calls=%fused_computation.29 | convolution fusion | flops 21454720 | bytes 5046816 | tf_op jit(solution)/shard_map/schgd,schpd->schgp/dot_general | solution.py:142
  44.0 4.2 %all-to-all-start.1 = ((f32[4,4,2,4]{3,2,1,0:T(2,128)}), f32[4,4,2,4]{3,2,1,0:T(2,128)S(1)}, u32[]{:S(2)}, u32[]{:S(2)}) async-start(f32[4,4,2,4]{3,2,1,0:T(2,128)} %get-tuple-element.49), calls=%async_computation.1 | async-start | bytes 32768 | tf_op jit(solution)/shard_map/all_to_all | solution.py:156
  48.2 3.2 %fusion = f32[4,4,2,4,128]{4,3,2,1,0:T(4,128)S(1)} fusion(bf16[4,4,2,576,128]{4,3,2,1,0:T(8,128)(2,1)} %bitcast.82, pred[4,4]{1,0:T(4,128)(4,1)S(1)} %compare_and_fusion.1, f32[4,4,2,4,576]{4,3,2,1,0:T(4,128)S(1)} %get-tuple-element.53, f32[4,4,2,4]{3,2,1,0:T(2,128)S(1)} %get-tuple-element.50, pred[4,4]{1,0:T(4,128)(4,1)S(1)} %bitcast.99), kind=kOutput, calls=%fused_computation.7 | convolution fusion | flops 21454848 | bytes 5079584 | tf_op jit(solution)/shard_map/schgp,schpd->schgd/dot_general | solution.py:152
  53.0 4.2 %all-to-all-start.3 = ((f32[4,4,2,4]{3,1,2,0:T(4,128)}), f32[4,4,2,4]{3,1,2,0:T(4,128)S(1)}, u32[]{:S(2)}, u32[]{:S(2)}) async-start(f32[4,4,2,4]{3,1,2,0:T(4,128)} %copy.141), calls=%async_computation.3 | async-start | bytes 32768 | tf_op jit(solution)/shard_map/all_to_all | solution.py:157
  57.5 4.5 %all-to-all-done.3 = f32[4,4,2,4]{3,1,2,0:T(4,128)S(1)} async-done(((f32[4,4,2,4]{3,1,2,0:T(4,128)}), f32[4,4,2,4]{3,1,2,0:T(4,128)S(1)}, u32[]{:S(2)}, u32[]{:S(2)}) %all-to-all-start.3) | async-done | bytes 544 | tf_op jit(solution)/shard_map/all_to_all | solution.py:157
  62.0 3.3 %all-to-all-start.2 = ((f32[4,4,2,4,128]{4,1,3,2,0:T(4,128)}), f32[4,4,2,4,128]{4,1,3,2,0:T(4,128)S(1)}, u32[]{:S(2)}, u32[]{:S(2)}) async-start(f32[4,4,2,4,128]{4,1,3,2,0:T(4,128)} %copy.131), calls=%async_computation.2 | async-start | bytes 131072 | tf_op jit(solution)/shard_map/all_to_all | solution.py:158
  65.6 1.8 all-gather.2
  67.6 1.8 all-gather.1
  70.4 2.0 fusion.13
  72.4 1.9 all-gather
  74.5 5.2 %fusion.31 = f32[8,4096]{1,0:T(8,128)} fusion(bf16[1024,4096]{1,0:T(8,128)(2,1)} %param.37, bf16[1,8,8,128]{3,2,1,0:T(8,128)(2,1)S(1)} %bitcast.89), kind=kOutput, calls=%fused_computation.61 | convolution fusion | flops 67108864 | bytes 8536064 | tf_op jit(solution)/shard_map/dot_general | solution.py:183
  81.1 35.1 %all-reduce.5.cloned.1.call-done = f32[8,4096]{1,0:T(8,128)} async-done(((f32[8,4096]{1,0:T(8,128)}), f32[8,4096]{1,0:T(8,128)}) %all-reduce.5.cloned.1.call-update) | async-done | bytes 131088
  118.3 41.7 %all-gather.3 = bf16[16,2,4096]{2,1,0:T(2,128)(2,1)S(1)} all-gather(bf16[1,2,4096]{2,1,0:T(2,128)(2,1)S(1)} %fusion.35), channel_id=1, replica_groups=mesh['group'=4,'depth'=2,'mp'=4] {'group','mp'}, dimensions={0}, use_global_device_ids=true | all-gather | bytes 278528 | tf_op jit(solution)/shard_map/all_gather | solution.py:191
  160.1 4.3 %fusion.63 = f32[32,896]{1,0:T(8,128)S(1)} fusion(bf16[32,4096]{1,0:T(8,128)(2,1)S(1)} %reshape.507, bf16[4096,896]{1,0:T(8,128)(2,1)} %param.39), kind=kOutput, calls=%fused_computation.153 | convolution fusion | flops 234881024 | bytes 7716864 | tf_op jit(solution)/shard_map/dot_general | solution.py:192
  164.4 8.5 %fusion.16 = f32[32,4096]{1,0:T(8,128)} fusion(bf16[896,4096]{1,0:T(8,128)(2,1)} %param.41, bf16[32,4096]{1,0:T(8,128)(2,1)S(1)} %reshape.507, bf16[4096,896]{1,0:T(8,128)(2,1)} %param.40, f32[32,896]{1,0:T(8,128)S(1)} %fusion.63), kind=kOutput, calls=%fused_computation.26 | convolution fusion | flops 469934080 | bytes 15581184 | tf_op jit(solution)/shard_map/dot_general | solution.py:197
  174.2 104.4 %all-reduce.7.cloned.1.call-done = f32[32,4096]{1,0:T(8,128)} async-done(((f32[32,4096]{1,0:T(8,128)}), f32[32,4096]{1,0:T(8,128)}) %all-reduce.7.cloned.1.call-update) | async-done | bytes 524304
  278.6 1.6 fusion.27
  (125 shorter events, 19.6 us)
Async XLA Ops:
  7.2 24.0 %copy-start = (bf16[8,2,576,128]{3,2,1,0:T(8,128)(2,1)S(1)}, bf16[8,2,576,128]{3,2,1,0:T(8,128)(2,1)}, u32[]{:S(2)}) copy-start(bf16[8,2,576,128]{3,2,1,0:T(8,128)(2,1)} %param.30) | copy-start | bytes 7077892
  7.2 23.2 %copy-start.2 = (bf16[16,8,128]{2,1,0:T(8,128)(2,1)S(1)}, bf16[16,8,128]{2,1,0:T(8,128)(2,1)}, u32[]{:S(2)}) copy-start(bf16[16,8,128]{2,1,0:T(8,128)(2,1)} %param.24) | copy-start | bytes 98308
  7.2 23.2 %copy-start.6 = (bf16[16,2,128]{2,1,0:T(2,128)(2,1)S(1)}, bf16[16,2,128]{2,1,0:T(2,128)(2,1)}, u32[]{:S(2)}) copy-start(bf16[16,2,128]{2,1,0:T(2,128)(2,1)} %param.25) | copy-start | bytes 24580
  16.6 22.8 %all-to-all-start = ((bf16[4,4,8,128]{3,2,1,0:T(8,128)(2,1)}), bf16[4,4,8,128]{3,2,1,0:T(8,128)(2,1)S(1)}, u32[]{:S(2)}, u32[]{:S(2)}) async-start(bf16[4,4,8,128]{3,2,1,0:T(8,128)(2,1)} %broadcast_select_fusion), calls=%async_computation | async-start | bytes 65536 | tf_op jit(solution)/shard_map/all_to_all | solution.py:137
  34.4 5.0 %copy-start.5 = (bf16[16,2,128]{2,1,0:T(2,128)(2,1)S(1)}, bf16[16,2,128]{2,1,0:T(2,128)(2,1)}, u32[]{:S(2)}) copy-start(bf16[16,2,128]{2,1,0:T(2,128)(2,1)} %param.26) | copy-start | bytes 24580
  44.0 9.0 %all-to-all-start.1 = ((f32[4,4,2,4]{3,2,1,0:T(2,128)}), f32[4,4,2,4]{3,2,1,0:T(2,128)S(1)}, u32[]{:S(2)}, u32[]{:S(2)}) async-start(f32[4,4,2,4]{3,2,1,0:T(2,128)} %get-tuple-element.49), calls=%async_computation.1 | async-start | bytes 32768 | tf_op jit(solution)/shard_map/all_to_all | solution.py:156
  53.0 8.9 %all-to-all-start.3 = ((f32[4,4,2,4]{3,1,2,0:T(4,128)}), f32[4,4,2,4]{3,1,2,0:T(4,128)S(1)}, u32[]{:S(2)}, u32[]{:S(2)}) async-start(f32[4,4,2,4]{3,1,2,0:T(4,128)} %copy.141), calls=%async_computation.3 | async-start | bytes 32768 | tf_op jit(solution)/shard_map/all_to_all | solution.py:157
  62.0 8.2 %all-to-all-start.2 = ((f32[4,4,2,4,128]{4,1,3,2,0:T(4,128)}), f32[4,4,2,4,128]{4,1,3,2,0:T(4,128)S(1)}, u32[]{:S(2)}, u32[]{:S(2)}) async-start(f32[4,4,2,4,128]{4,1,3,2,0:T(4,128)} %copy.131), calls=%async_computation.2 | async-start | bytes 131072 | tf_op jit(solution)/shard_map/all_to_all | solution.py:158
  65.2 51.0 %all-reduce.5.cloned.1.call-start = ((), (), s32[]{:S(2)}) async-start(), calls=%async_computation.4 | async-start | bytes 262144
  74.4 5.3 %copy-start.3 = (bf16[8,8,128]{2,1,0:T(8,128)(2,1)}, bf16[8,8,128]{2,1,0:T(8,128)(2,1)S(1)}, u32[]{:S(2)}) copy-start(bf16[8,8,128]{2,1,0:T(8,128)(2,1)S(1)} %fusion.28) | copy-start | bytes 49156
  74.5 5.3 %copy-start.8 = (u32[32]{0:T(128)S(1)}, u32[32]{0:T(128)}, u32[]{:S(2)}) copy-start(u32[32]{0:T(128)} %constant.204) | copy-start | bytes 388
  74.5 41.7 %copy-start.1 = (bf16[2,4096]{1,0:T(2,128)(2,1)S(1)}, bf16[2,4096]{1,0:T(2,128)(2,1)}, u32[]{:S(2)}) copy-start(bf16[2,4096]{1,0:T(2,128)(2,1)} %param.23) | copy-start | bytes 49156
  74.5 42.8 %copy-start.4 = (f32[4096]{0:T(1024)S(1)}, f32[4096]{0:T(1024)}, u32[]{:S(2)}) copy-start(f32[4096]{0:T(1024)} %param.38) | copy-start | bytes 49156
  79.8 198.8 %all-reduce.7.cloned.1.call-start = ((), (), s32[]{:S(2)}) async-start(), calls=%async_computation.5 | async-start | bytes 1048576
  164.4 8.6 %copy-start.7 = (u32[32]{0:T(128)S(1)}, u32[32]{0:T(128)}, u32[]{:S(2)}) copy-start(u32[32]{0:T(128)} %constant.208) | copy-start | bytes 388
Sparse Core Ops, SparseCore 0:
  79.9 36.2 all-reduce.4
  173.0 105.4 all-reduce.6
where the time goes:
time: 288 us; the launch traced here: 287 us
  waiting for transfers between devices  144 us (50%)
  blocking collectives  47.2 us (16%)
  matrix products  30.2 us (10%)
  local copies, waits for them, and re-layouts  21.6 us (8%)
  starting transfers between devices  16.9 us (6%)
  between operations  15.7 us (5%)
  other arithmetic  11.2 us (4%)
    unnamed x4, waiting for transfers between devices  140 us
    all_gather x1, blocking collectives, on_device(): piece = lax.all_gather(normed, ('group', 'mp'), axis=0, tiled=True)  41.7 us
    dot_general x1, matrix products, on_device(): jnp.dot(picked_rows, down_weight, preferred_element_type=jnp.float32)  8.51 us
  transfers between devices with their start and end apart: 6, of which 3 were waited for; matrix products, arithmetic and copies ran while one was open for 9% of the time, Pallas kernels for 0%

commit v1 on v0

--- a/solution.py
+++ b/solution.py
@@ -188,7 +188,10 @@
     residual = states.astype(jnp.float32) + projected
     spread = jnp.mean(residual * residual, axis=-1, keepdims=True)
     normed = (residual * lax.rsqrt(spread + NORM_EPSILON) * norm_gain).astype(jnp.bfloat16)
-    piece = lax.all_gather(normed, ("group", "mp"), axis=0, tiled=True)
+    piece = jnp.concatenate(
+        lax.all_to_all(jnp.stack([normed] * lax.axis_size(("group", "mp"))), ("group", "mp"), 0, 0),
+        axis=0,
+    )
     gate_term = jnp.dot(piece, gate_weight, preferred_element_type=jnp.float32)
     up_term = jnp.dot(piece, up_weight, preferred_element_type=jnp.float32)
     hidden = (jax.nn.silu(gate_term) * up_term).astype(jnp.bfloat16)

time: 288 us -> 262 us (0.910)
  blocking collectives: 47.2 us -> 19.5 us
    all_gather x1 -> x0, blocking collectives: 41.7 us -> none  [on_device(): piece = lax.all_gather(normed, ('group', 'mp'), axis=0, tiled=True)]
    all_to_all x0 -> x1, blocking collectives: none -> 13.9 us  [on_device(): lax.all_to_all(jnp.stack([normed] * lax.axis_size(('group', 'mp'))), ('gr...]
  transfers between devices with their start and end apart: 6 -> 6, of which waited for: 3 -> 3; matrix products, arithmetic and copies ran while one was open for 9% -> 10% of each run, Pallas kernels for 0% -> 0%
where the time goes in v1:
time: 262 us; the launch traced here: 261 us
  waiting for transfers between devices  145 us (55%)
  matrix products  30.2 us (12%)
  local copies, waits for them, and re-layouts  21.8 us (8%)
  blocking collectives  19.5 us (7%)
  starting transfers between devices  16.9 us (6%)
  between operations  15.7 us (6%)
  other arithmetic  11.2 us (4%)
    unnamed x4, waiting for transfers between devices  141 us
    all_to_all x1, blocking collectives, on_device(): lax.all_to_all(jnp.stack([normed] * lax.axis_size(('group', 'mp'))), ('gr...  13.9 us
    dot_general x1, matrix products, on_device(): jnp.dot(picked_rows, down_weight, preferred_element_type=jnp.float32)  8.51 us
    all_gather x3, blocking collectives, merged(): gathered = jax.tree.map(lambda a: lax.all_gather(a, axis), part)  5.54 us
  transfers between devices with their start and end apart: 6, of which 3 were waited for; matrix products, arithmetic and copies ran while one was open for 10% of the time, Pallas kernels for 0%

profile of v1, /device:TPU:0, one launch (start us, length us, event | category | flops | bytes accessed | tf_op | source)
XLA Modules:
  0.0 260.5 jit_solution(16473309175646977907)
XLA Ops:
  8.8 1.3 gather_fusion.4
  14.6 1.3 gather_fusion.2
  16.6 5.2 %all-to-all-start = ((bf16[4,4,8,128]{3,2,1,0:T(8,128)(2,1)}), bf16[4,4,8,128]{3,2,1,0:T(8,128)(2,1)S(1)}, u32[]{:S(2)}, u32[]{:S(2)}) async-start(bf16[4,4,8,128]{3,2,1,0:T(8,128)(2,1)} %broadcast_select_fusion), calls=%async_computation | async-start | bytes 65536 | tf_op jit(solution)/shard_map/all_to_all | solution.py:137
  24.1 1.4 gather_fusion.1
  27.9 2.3 select_reduce_fusion.1
  31.1 3.3 %gather_fusion.5 = bf16[16,2,576,128]{3,2,1,0:T(8,128)(2,1)} fusion(bf16[8,2,576,128]{3,2,1,0:T(8,128)(2,1)S(1)} %copy-done, s32[1024]{0:T(1024)S(1)} %pad_clamp_fusion), kind=kCustom, calls=%fused_computation.1.clone | custom fusion | bytes 9437248 | tf_op jit(solution)/shard_map/jit(_take)/gather | solution.py:139
  34.5 5.0 %gather_fusion.6 = bf16[16,2,576,128]{3,2,1,0:T(8,128)(2,1)} fusion(bf16[8,2,576,128]{3,2,1,0:T(8,128)(2,1)} %param.31, s32[1024]{0:T(1024)S(1)} %pad_clamp_fusion), kind=kCustom, calls=%fused_computation.3.clone | custom fusion | bytes 9437248 | tf_op jit(solution)/shard_map/jit(_take)/gather | solution.py:140
  39.4 4.0 %select_reduce_fusion = (f32[4,4,2,4]{3,2,1,0:T(2,128)S(1)}, f32[4,4,2,4,576]{4,3,2,1,0:T(4,128)S(1)}) fusion(pred[4,4]{1,0:T(4,128)(4,1)S(1)} %bitcast.96, bf16[4,4,2,4,128]{4,3,2,1,0:T(4,128)(2,1)S(1)} %bitcast.89, bf16[4,4,2,576,128]{4,3,2,1,0:T(8,128)(2,1)} %bitcast.81, pred[4,4]{1,0:T(4,128)(4,1)S(1)} %compare_and_fusion.1), kind=kOutput, calls=%fused_computation.29 | convolution fusion | flops 21454720 | bytes 5046816 | tf_op jit(solution)/shard_map/schgd,schpd->schgp/dot_general | solution.py:142
  44.0 4.2 %all-to-all-start.1 = ((f32[4,4,2,4]{3,2,1,0:T(2,128)}), f32[4,4,2,4]{3,2,1,0:T(2,128)S(1)}, u32[]{:S(2)}, u32[]{:S(2)}) async-start(f32[4,4,2,4]{3,2,1,0:T(2,128)} %get-tuple-element.49), calls=%async_computation.1 | async-start | bytes 32768 | tf_op jit(solution)/shard_map/all_to_all | solution.py:156
  48.2 3.2 %fusion = f32[4,4,2,4,128]{4,3,2,1,0:T(4,128)S(1)} fusion(bf16[4,4,2,576,128]{4,3,2,1,0:T(8,128)(2,1)} %bitcast.80, pred[4,4]{1,0:T(4,128)(4,1)S(1)} %compare_and_fusion.1, f32[4,4,2,4,576]{4,3,2,1,0:T(4,128)S(1)} %get-tuple-element.53, f32[4,4,2,4]{3,2,1,0:T(2,128)S(1)} %get-tuple-element.50, pred[4,4]{1,0:T(4,128)(4,1)S(1)} %bitcast.97), kind=kOutput, calls=%fused_computation.7 | convolution fusion | flops 21454848 | bytes 5079584 | tf_op jit(solution)/shard_map/schgp,schpd->schgd/dot_general | solution.py:152
  53.0 4.2 %all-to-all-start.3 = ((f32[4,4,2,4]{3,1,2,0:T(4,128)}), f32[4,4,2,4]{3,1,2,0:T(4,128)S(1)}, u32[]{:S(2)}, u32[]{:S(2)}) async-start(f32[4,4,2,4]{3,1,2,0:T(4,128)} %copy.141), calls=%async_computation.3 | async-start | bytes 32768 | tf_op jit(solution)/shard_map/all_to_all | solution.py:157
  57.5 4.5 %all-to-all-done.3 = f32[4,4,2,4]{3,1,2,0:T(4,128)S(1)} async-done(((f32[4,4,2,4]{3,1,2,0:T(4,128)}), f32[4,4,2,4]{3,1,2,0:T(4,128)S(1)}, u32[]{:S(2)}, u32[]{:S(2)}) %all-to-all-start.3) | async-done | bytes 544 | tf_op jit(solution)/shard_map/all_to_all | solution.py:157
  62.0 3.3 %all-to-all-start.2 = ((f32[4,4,2,4,128]{4,1,3,2,0:T(4,128)}), f32[4,4,2,4,128]{4,1,3,2,0:T(4,128)S(1)}, u32[]{:S(2)}, u32[]{:S(2)}) async-start(f32[4,4,2,4,128]{4,1,3,2,0:T(4,128)} %copy.131), calls=%async_computation.2 | async-start | bytes 131072 | tf_op jit(solution)/shard_map/all_to_all | solution.py:158
  65.6 1.8 all-gather.2
  67.6 1.8 all-gather.1
  70.4 2.0 fusion.13
  72.4 1.9 all-gather
  74.5 5.2 %fusion.31 = f32[8,4096]{1,0:T(8,128)} fusion(bf16[1024,4096]{1,0:T(8,128)(2,1)} %param.37, bf16[1,8,8,128]{3,2,1,0:T(8,128)(2,1)S(1)} %bitcast.87), kind=kOutput, calls=%fused_computation.61 | convolution fusion | flops 67108864 | bytes 8536064 | tf_op jit(solution)/shard_map/dot_general | solution.py:183
  81.1 35.1 %all-reduce.5.cloned.1.call-done = f32[8,4096]{1,0:T(8,128)} async-done(((f32[8,4096]{1,0:T(8,128)}), f32[8,4096]{1,0:T(8,128)}) %all-reduce.5.cloned.1.call-update) | async-done | bytes 131088
  118.5 13.9 %all_to_all.25 = bf16[16,2,4096]{2,1,0:T(2,128)(2,1)S(1)} all-to-all(bf16[16,2,4096]{2,1,0:T(2,128)(2,1)S(1)} %stack.2), channel_id=1, replica_groups=mesh['group'=4,'depth'=2,'mp'=4] {'group','mp'}, dimensions={0} | all-to-all | bytes 524288 | tf_op jit(solution)/shard_map/all_to_all | solution.py:192
  132.5 4.3 %fusion.62 = f32[32,896]{1,0:T(8,128)S(1)} fusion(bf16[32,4096]{1,0:T(8,128)(2,1)S(1)} %reshape.433, bf16[4096,896]{1,0:T(8,128)(2,1)} %param.39), kind=kOutput, calls=%fused_computation.152 | convolution fusion | flops 234881024 | bytes 7716864 | tf_op jit(solution)/shard_map/dot_general | solution.py:195
  136.8 8.5 %fusion.16 = f32[32,4096]{1,0:T(8,128)} fusion(bf16[896,4096]{1,0:T(8,128)(2,1)} %param.41, bf16[32,4096]{1,0:T(8,128)(2,1)S(1)} %reshape.433, bf16[4096,896]{1,0:T(8,128)(2,1)} %param.40, f32[32,896]{1,0:T(8,128)S(1)} %fusion.62), kind=kOutput, calls=%fused_computation.26 | convolution fusion | flops 469934080 | bytes 15581184 | tf_op jit(solution)/shard_map/dot_general | solution.py:200
  146.6 105.5 %all-reduce.7.cloned.1.call-done = f32[32,4096]{1,0:T(8,128)} async-done(((f32[32,4096]{1,0:T(8,128)}), f32[32,4096]{1,0:T(8,128)}) %all-reduce.7.cloned.1.call-update) | async-done | bytes 524304
  252.1 1.6 fusion.27
  (126 shorter events, 19.8 us)
Async XLA Ops:
  7.2 24.0 %copy-start = (bf16[8,2,576,128]{3,2,1,0:T(8,128)(2,1)S(1)}, bf16[8,2,576,128]{3,2,1,0:T(8,128)(2,1)}, u32[]{:S(2)}) copy-start(bf16[8,2,576,128]{3,2,1,0:T(8,128)(2,1)} %param.30) | copy-start | bytes 7077892
  7.2 23.2 %copy-start.2 = (bf16[16,8,128]{2,1,0:T(8,128)(2,1)S(1)}, bf16[16,8,128]{2,1,0:T(8,128)(2,1)}, u32[]{:S(2)}) copy-start(bf16[16,8,128]{2,1,0:T(8,128)(2,1)} %param.24) | copy-start | bytes 98308
  7.2 23.2 %copy-start.6 = (bf16[16,2,128]{2,1,0:T(2,128)(2,1)S(1)}, bf16[16,2,128]{2,1,0:T(2,128)(2,1)}, u32[]{:S(2)}) copy-start(bf16[16,2,128]{2,1,0:T(2,128)(2,1)} %param.25) | copy-start | bytes 24580
  16.6 22.8 %all-to-all-start = ((bf16[4,4,8,128]{3,2,1,0:T(8,128)(2,1)}), bf16[4,4,8,128]{3,2,1,0:T(8,128)(2,1)S(1)}, u32[]{:S(2)}, u32[]{:S(2)}) async-start(bf16[4,4,8,128]{3,2,1,0:T(8,128)(2,1)} %broadcast_select_fusion), calls=%async_computation | async-start | bytes 65536 | tf_op jit(solution)/shard_map/all_to_all | solution.py:137
  34.4 5.0 %copy-start.5 = (bf16[16,2,128]{2,1,0:T(2,128)(2,1)S(1)}, bf16[16,2,128]{2,1,0:T(2,128)(2,1)}, u32[]{:S(2)}) copy-start(bf16[16,2,128]{2,1,0:T(2,128)(2,1)} %param.26) | copy-start | bytes 24580
  44.0 9.0 %all-to-all-start.1 = ((f32[4,4,2,4]{3,2,1,0:T(2,128)}), f32[4,4,2,4]{3,2,1,0:T(2,128)S(1)}, u32[]{:S(2)}, u32[]{:S(2)}) async-start(f32[4,4,2,4]{3,2,1,0:T(2,128)} %get-tuple-element.49), calls=%async_computation.1 | async-start | bytes 32768 | tf_op jit(solution)/shard_map/all_to_all | solution.py:156
  53.0 8.9 %all-to-all-start.3 = ((f32[4,4,2,4]{3,1,2,0:T(4,128)}), f32[4,4,2,4]{3,1,2,0:T(4,128)S(1)}, u32[]{:S(2)}, u32[]{:S(2)}) async-start(f32[4,4,2,4]{3,1,2,0:T(4,128)} %copy.141), calls=%async_computation.3 | async-start | bytes 32768 | tf_op jit(solution)/shard_map/all_to_all | solution.py:157
  62.0 8.2 %all-to-all-start.2 = ((f32[4,4,2,4,128]{4,1,3,2,0:T(4,128)}), f32[4,4,2,4,128]{4,1,3,2,0:T(4,128)S(1)}, u32[]{:S(2)}, u32[]{:S(2)}) async-start(f32[4,4,2,4,128]{4,1,3,2,0:T(4,128)} %copy.131), calls=%async_computation.2 | async-start | bytes 131072 | tf_op jit(solution)/shard_map/all_to_all | solution.py:158
  65.2 51.0 %all-reduce.5.cloned.1.call-start = ((), (), s32[]{:S(2)}) async-start(), calls=%async_computation.5 | async-start | bytes 262144
  74.4 5.3 %copy-start.3 = (bf16[8,8,128]{2,1,0:T(8,128)(2,1)}, bf16[8,8,128]{2,1,0:T(8,128)(2,1)S(1)}, u32[]{:S(2)}) copy-start(bf16[8,8,128]{2,1,0:T(8,128)(2,1)S(1)} %fusion.28) | copy-start | bytes 49156
  74.5 5.3 %copy-start.8 = (u32[32]{0:T(128)S(1)}, u32[32]{0:T(128)}, u32[]{:S(2)}) copy-start(u32[32]{0:T(128)} %constant.204) | copy-start | bytes 388
  74.5 41.7 %copy-start.1 = (bf16[2,4096]{1,0:T(2,128)(2,1)S(1)}, bf16[2,4096]{1,0:T(2,128)(2,1)}, u32[]{:S(2)}) copy-start(bf16[2,4096]{1,0:T(2,128)(2,1)} %param.23) | copy-start | bytes 49156
  74.5 42.8 %copy-start.4 = (f32[4096]{0:T(1024)S(1)}, f32[4096]{0:T(1024)}, u32[]{:S(2)}) copy-start(f32[4096]{0:T(1024)} %param.38) | copy-start | bytes 49156
  79.8 172.3 %all-reduce.7.cloned.1.call-start = ((), (), s32[]{:S(2)}) async-start(), calls=%async_computation.6 | async-start | bytes 1048576
  136.8 8.6 %copy-start.7 = (u32[32]{0:T(128)S(1)}, u32[32]{0:T(128)}, u32[]{:S(2)}) copy-start(u32[32]{0:T(128)} %constant.208) | copy-start | bytes 388
Sparse Core Ops, SparseCore 0:
  79.9 36.2 all-reduce.4
  145.5 106.5 all-reduce.6
